TPU v7x, 32 devices: a whole 2x2x4 slice. The times are simulated.
32 devices in a mesh: row: 8 (over z, x), col: 4 (over y, core).
Axes of the slice: x: 2, y: 2, z: 4, core: 2. Of those that a mesh axis runs over, the one named last changes fastest.
Arguments:
- density_first: bfloat16 [12288, 12288], P('row', 'col'), may hold values from -0.0068359375 to 0.0068359375
- density_second: bfloat16 [12288, 12288], P('row', 'col'), may hold values from -0.0068359375 to 0.0068359375
- basis: bfloat16 [64, 4096, 896], P(('row', 'col')), may hold values from -6 to 6
- tile_list: int32 [64, 7], P(('row', 'col')), may hold values from 0 to 95, as said below
- tile_count: int32 [64], P(('row', 'col')), may hold values from 5 to 7, as said below
- point_count: int32 [64], P(('row', 'col')), may hold values from 1024 to 4096, as said below
- offsets: float32 [3, 64, 4096], P(None, ('row', 'col')), may hold values from -5 to 5
- weights: float32 [64, 4096], P(('row', 'col')), may hold values from 0.05 to 1
- atom_of_point: int32 [64, 4096], P(('row', 'col')), may hold values from 0 to 1023, as said below
Outputs:
- density: float32 [2, 64, 4096], P(None, ('row', 'col'))
- moments: float32 [2, 9, 1024], replicated
Inputs may be any that keep to these rules, and one draw needn't show every extreme that they name: `tile_list`: the 7 tile numbers of each batch are 7 consecutive numbers in some order. `tile_count`: some batch has 7. `point_count`: some batch has 4096. `atom_of_point`: the points of batch g belong to atoms (g * 16 + j) mod 1024 with j from 0 to 7.
All inputs are finite; a program needn't handle non-finite values.
Results may differ from a plain program's by a relative error of at most 0.0003.
Values may be sent and summed in bfloat16 or wider, within the bound.
A program may use at most 192 MiB of HBM per device.

v0:
```python
import functools

import jax
import jax.numpy as jnp
from jax import lax
from jax.experimental import pallas as pl
from jax.experimental.pallas import tpu as pltpu
from jax.sharding import PartitionSpec as P

TILE = 128
ATOMS = 1024
SPREAD = 8
TERMS = 24


def share_kernel(row_count, col_count, mine, every, held, send_sem, recv_sem, self_sem):
    peers = row_count * col_count
    me = lax.axis_index("row") * col_count + lax.axis_index("col")
    barrier = pltpu.get_barrier_semaphore()

    def device(index):
        return (index // col_count, index % col_count)

    def greet(hop, carry):
        pl.semaphore_signal(
            barrier, inc=1, device_id=device((me + hop) % peers),
            device_id_type=pl.DeviceIdType.MESH,
        )
        return carry

    def copy(hop, place):
        return pltpu.make_async_remote_copy(
            src_ref=mine,
            dst_ref=held.at[place],
            send_sem=send_sem.at[hop],
            recv_sem=recv_sem.at[hop],
            device_id=device((me + hop) % peers),
            device_id_type=pl.DeviceIdType.MESH,
        )

    def send(hop, carry):
        copy(hop, me).start()
        return carry

    def finish(hop, carry):
        copy(hop, (me + peers - hop) % peers).wait_recv()
        copy(hop, me).wait_send()
        return carry

    lax.fori_loop(1, peers, greet, 0)
    own = pltpu.make_async_copy(mine, held.at[me], self_sem)
    own.start()
    pl.semaphore_wait(barrier, peers - 1)
    lax.fori_loop(1, peers, send, 0)
    own.wait()
    lax.fori_loop(1, peers, finish, 0)
    every[...] = held[...]


def share(mine, row_count, col_count, collective_id):
    peers = row_count * col_count
    shape = (peers,) + mine.shape
    return pl.pallas_call(
        functools.partial(share_kernel, row_count, col_count),
        out_shape=jax.ShapeDtypeStruct(shape, mine.dtype),
        in_specs=[pl.BlockSpec(memory_space=pltpu.VMEM)],
        out_specs=pl.BlockSpec(memory_space=pltpu.VMEM),
        scratch_shapes=[
            pltpu.VMEM(shape, mine.dtype),
            pltpu.SemaphoreType.DMA((peers,)),
            pltpu.SemaphoreType.DMA((peers,)),
            pltpu.SemaphoreType.DMA,
        ],
        compiler_params=pltpu.CompilerParams(collective_id=collective_id, has_side_effects=True),
        name="share",
    )(mine)


def pack_kernel(row_at, col_at, first, second, out, sem):
    height, width = out.shape[2], out.shape[3]

    def issue(peer, carry):
        rows = pl.ds(pl.multiple_of(row_at[peer] * TILE, TILE), height)
        cols = pl.ds(pl.multiple_of(col_at[peer] * TILE, TILE), width)
        pltpu.make_async_copy(first.at[rows, cols], out.at[peer, 0], sem).start()
        pltpu.make_async_copy(second.at[rows, cols], out.at[peer, 1], sem).start()
        return carry

    lax.fori_loop(0, out.shape[0], issue, 0)
    pltpu.make_async_copy(out, out, sem).wait()


def pack(row_at, col_at, first, second, height, width):
    peers = row_at.shape[0]
    shape = (peers, 2, height, width)
    return pl.pallas_call(
        pack_kernel,
        out_shape=jax.ShapeDtypeStruct(shape, first.dtype),
        in_specs=[
            pl.BlockSpec(memory_space=pltpu.SMEM),
            pl.BlockSpec(memory_space=pltpu.SMEM),
            pl.BlockSpec(memory_space=pl.ANY),
            pl.BlockSpec(memory_space=pl.ANY),
        ],
        out_specs=pl.BlockSpec(memory_space=pltpu.VMEM),
        scratch_shapes=[pltpu.SemaphoreType.DMA],
        cost_estimate=pl.CostEstimate(
            flops=0, bytes_accessed=4 * peers * height * width * 2, transcendentals=0
        ),
        name="pack",
    )(row_at, col_at, first, second)


def density_kernel(
    run, batch, counts, peer_at, row_slot, col_slot, arrived, basis, geometry, atoms,
    density, moments, block, sem,
):
    step = pl.program_id(0)
    points = basis.shape[1]
    span = run * TILE
    live_tiles = counts[0]
    live_points = counts[1]

    @pl.when(step == 0)
    def _():
        def issue(index, carry):
            k = index // run
            l = index % run
            peer = peer_at[index]
            rows = pl.ds(pl.multiple_of(row_slot[k] * TILE, TILE), TILE)
            cols = pl.ds(pl.multiple_of(col_slot[l] * TILE, TILE), TILE)
            to_rows = pl.ds(pl.multiple_of(k * TILE, TILE), TILE)
            for d in range(2):
                to_cols = pl.ds(pl.multiple_of(d * span + l * TILE, TILE), TILE)
                pltpu.make_async_copy(
                    arrived.at[peer, d, rows, cols], block.at[to_rows, to_cols], sem
                ).start()
            return carry

        lax.fori_loop(0, run * run, issue, 0)
        moments[...] = jnp.zeros_like(moments)
        pltpu.make_async_copy(block, block, sem).wait()
        for k in range(run):

            @pl.when(k >= live_tiles)
            def _():
                for l in range(2 * run):
                    block[k * TILE:(k + 1) * TILE, l * TILE:(l + 1) * TILE] = jnp.zeros(
                        (TILE, TILE), block.dtype
                    )
                for d in range(2):
                    for l in range(run):
                        first = d * span + k * TILE
                        block[l * TILE:(l + 1) * TILE, first:first + TILE] = jnp.zeros(
                            (TILE, TILE), block.dtype
                        )

    @pl.when(step * points >= live_points)
    def _():
        density[...] = jnp.zeros_like(density)

    @pl.when(step * points < live_points)
    def _():
        place = step * points + lax.broadcasted_iota(jnp.int32, (1, points), 1)
        live = place < live_points
        fewest = max(run - 2, 1)
        for used in range(fewest, run + 1):
            width = used * TILE

            @pl.when(live_tiles <= used if used == fewest else live_tiles == used)
            def _():
                values = basis[0, :, 0:width]
                parts = []
                for d in range(2):
                    product = jnp.dot(
                        values, block[0:width, d * span:d * span + width],
                        preferred_element_type=jnp.float32,
                    )
                    total = None
                    for l in range(used):
                        part = product[:, l * TILE:(l + 1) * TILE] * values[
                            :, l * TILE:(l + 1) * TILE
                        ].astype(jnp.float32)
                        total = part if total is None else total + part
                    row = jnp.sum(total.T, axis=0, keepdims=True)
                    parts.append(jnp.where(live, row, 0.0))
                density[...] = jnp.concatenate(parts, axis=0)

        rows = [density[d:d + 1, :] for d in range(2)]
        x = geometry[0:1, :]
        y = geometry[1:2, :]
        z = geometry[2:3, :]
        w = geometry[3:4, :]
        r2 = x * x + y * y + z * z
        weighted = [
            w, w * x, w * y, w * z, w * (x * y), w * (y * z),
            w * (3.0 * z * z - r2), w * (x * z), w * (x * x - y * y),
        ]
        terms = [rows[d] * item for d in range(2) for item in weighted]
        terms += [jnp.zeros((1, points), jnp.float32)] * (TERMS - len(terms))
        stacked = jnp.concatenate(terms, axis=0)
        atom = atoms[...]
        for j in range(SPREAD):
            chosen = jnp.where(atom == j, stacked, 0.0)
            total = None
            for c in range(points // TILE):
                part = chosen[:, c * TILE:(c + 1) * TILE]
                total = part if total is None else total + part
            moments[j] = moments[j] + total


def density_of(batch, counts, peer_at, row_slot, col_slot, arrived, basis, geometry, atoms):
    points, span = basis.shape[1], basis.shape[2]
    run = span // TILE
    chunk = min(512, points)
    grid = points // chunk

    def basis_map(i, counts, *_):
        last = jnp.maximum((counts[1] + chunk - 1) // chunk - 1, 0)
        return (batch, jnp.minimum(i, last), 0)

    return pl.pallas_call(
        functools.partial(density_kernel, run, batch),
        grid_spec=pltpu.PrefetchScalarGridSpec(
            num_scalar_prefetch=4,
            grid=(grid,),
            in_specs=[
                pl.BlockSpec(memory_space=pl.ANY),
                pl.BlockSpec((1, chunk, span), basis_map),
                pl.BlockSpec((4, chunk), lambda i, *_: (0, i)),
                pl.BlockSpec((1, chunk), lambda i, *_: (0, i)),
            ],
            out_specs=[
                pl.BlockSpec((2, chunk), lambda i, *_: (0, i)),
                pl.BlockSpec((SPREAD, TERMS, TILE), lambda i, *_: (0, 0, 0)),
            ],
            scratch_shapes=[
                pltpu.VMEM((span, 2 * span), basis.dtype),
                pltpu.SemaphoreType.DMA,
            ],
        ),
        out_shape=[
            jax.ShapeDtypeStruct((2, points), jnp.float32),
            jax.ShapeDtypeStruct((SPREAD, TERMS, TILE), jnp.float32),
        ],
        compiler_params=pltpu.CompilerParams(
            dimension_semantics=("arbitrary",), vmem_limit_bytes=60 * 1024 * 1024
        ),
        cost_estimate=pl.CostEstimate(
            flops=4 * points * span * span,
            bytes_accessed=2 * points * span + 4 * span * span,
            transcendentals=0,
        ),
        name="density",
    )(counts, peer_at, row_slot, col_slot, arrived, basis, geometry, atoms)


def local(
    density_first,
    density_second,
    basis,
    tile_list,
    tile_count,
    point_count,
    offsets,
    weights,
    atom_of_point,
):
    row_count = lax.axis_size("row")
    col_count = lax.axis_size("col")
    peers = row_count * col_count
    local_rows = density_first.shape[0] // TILE
    local_cols = density_first.shape[1] // TILE
    batches_dev, run = tile_list.shape
    row_slots = min(-(-run // row_count), local_rows)
    col_slots = min(-(-run // col_count), local_cols)
    my_row = lax.axis_index("row")
    my_col = lax.axis_index("col")
    me = my_row * col_count + my_col
    own_start = jnp.min(tile_list, axis=1)
    padded = jnp.pad(own_start[None, :], ((0, 0), (0, TILE - batches_dev)))
    starts = share(padded, row_count, col_count, 0)[:, 0, :batches_dev]

    def first_held(start, owner, parts, held, slots):
        first = (start + (owner - start) % parts) // parts
        return jnp.minimum(first, held - slots).astype(jnp.int32)

    row_at = first_held(starts, my_row, row_count, local_rows, row_slots)
    col_at = first_held(starts, my_col, col_count, local_cols, col_slots)

    moved = [
        lax.all_to_all(
            pack(
                row_at[:, b], col_at[:, b], density_first, density_second,
                row_slots * TILE, col_slots * TILE,
            ),
            ("row", "col"), split_axis=0, concat_axis=0, tiled=True,
        )
        for b in range(batches_dev)
    ]

    own = own_start[:, None]
    owner_row = tile_list % row_count
    owner_col = tile_list % col_count
    row_slot = tile_list // row_count - first_held(own, owner_row, row_count, local_rows, row_slots)
    col_slot = tile_list // col_count - first_held(own, owner_col, col_count, local_cols, col_slots)
    peer_at = (owner_row[:, :, None] * col_count + owner_col[:, None, :]).reshape(batches_dev, -1)
    stride = ATOMS // (peers * batches_dev)
    base = (me * batches_dev + jnp.arange(batches_dev, dtype=jnp.int32)) * stride
    atom_slot = (atom_of_point - base[:, None]) % ATOMS
    geometry = jnp.concatenate([offsets, weights[None]], axis=0)

    densities = []
    partials = []
    for b in range(batches_dev):
        density, partial = density_of(
            b, jnp.stack([tile_count[b], point_count[b]]), peer_at[b], row_slot[b], col_slot[b],
            moved[b], basis, geometry[:, b], atom_slot[b:b + 1],
        )
        densities.append(density)
        partials.append(jnp.sum(partial, axis=2))
    density = jnp.stack(densities, axis=1)
    mine = jnp.concatenate(partials, axis=1)
    mine = jnp.pad(mine, ((0, 0), (0, -mine.shape[1] % TILE)))
    every = share(mine, row_count, col_count, 1)
    every = jnp.stack(
        [every[:, :, b * TERMS:b * TERMS + 18] for b in range(batches_dev)], axis=1
    ).reshape(peers * batches_dev, SPREAD, 18)
    blocks = -(-SPREAD // stride)
    every = jnp.pad(every, ((0, 0), (0, blocks * stride - SPREAD), (0, 0)))
    total = None
    for q in range(blocks):
        part = every[:, q * stride:(q + 1) * stride].reshape(ATOMS, 18)
        part = jnp.roll(part, q * stride, axis=0)
        total = part if total is None else total + part
    return density, total.T.reshape(2, 9, ATOMS)


def solution(mesh):
    placed = (
        P("row", "col"),
        P("row", "col"),
        P(("row", "col"), None, None),
        P(("row", "col"), None),
        P(("row", "col")),
        P(("row", "col")),
        P(None, ("row", "col"), None),
        P(("row", "col"), None),
        P(("row", "col"), None),
    )
    return jax.shard_map(
        local,
        mesh=mesh,
        in_specs=placed,
        out_specs=(P(None, ("row", "col"), None), P()),
        check_vma=False,
    )
```

profile of v0, /device:TPU:0, one launch (start us, length us, event | category | flops | bytes accessed | tf_op | source)
XLA Modules:
  0.0 254.9 jit_solution(4435170023396338899)
XLA Ops:
  0.6 0.8 reduce_min.9
  1.4 0.5 pad.12.mine
  2.0 11.4 %share.2 = s32[32,1,128]{2,1,0:T(1,128)} custom-call(s32[1,128]{1,0:T(1,128)} %pad.12.mine), custom_call_target="tpu_custom_call" | custom-call | tf_op jit(solution)/shard_map/share/pallas_call | solution.py:63
  13.4 0.8 copy.14
  14.2 0.5 slice_bitcast_fusion.6
  14.7 5.3 %pack.2 = bf16[32,2,128,256]{3,2,1,0:T(8,128)(2,1)} custom-call(s32[32]{0:T(128)} %get-tuple-element.45.row_at, s32[32]{0:T(128)} %get-tuple-element.25.col_at, bf16[1536,3072]{1,0:T(8,128)(2,1)} %first.3, bf16[1536,3072]{1,0:T(8,128)(2,1)} %second.3), custom_call_target="tpu_custom_call" | custom-call | bytes 8388608 | tf_op jit(solution)/shard_map/pack/pallas_call | solution.py:96
  20.1 5.0 %all-to-all-start = ((bf16[32,2,128,256]{3,2,1,0:T(8,128)(2,1)}), bf16[32,2,128,256]{3,2,1,0:T(8,128)(2,1)}, u32[]{:S(2)}, u32[]{:S(2)}) async-start(bf16[32,2,128,256]{3,2,1,0:T(8,128)(2,1)} %pack.2), calls=%async_computation | async-start | bytes 8388608 | tf_op jit(solution)/shard_map/all_to_all | solution.py:292
  25.1 5.4 %pack.3 = bf16[32,2,128,256]{3,2,1,0:T(8,128)(2,1)} custom-call(s32[32]{0:T(128)} %get-tuple-element.44.row_at, s32[32]{0:T(128)} %get-tuple-element.26.col_at, bf16[1536,3072]{1,0:T(8,128)(2,1)} %first.3, bf16[1536,3072]{1,0:T(8,128)(2,1)} %second.3), custom_call_target="tpu_custom_call" | custom-call | bytes 8388608 | tf_op jit(solution)/shard_map/pack/pallas_call | solution.py:96
  30.6 88.8 %all-to-all-done.arrived = bf16[32,2,128,256]{3,2,1,0:T(8,128)(2,1)} async-done(((bf16[32,2,128,256]{3,2,1,0:T(8,128)(2,1)}), bf16[32,2,128,256]{3,2,1,0:T(8,128)(2,1)}, u32[]{:S(2)}, u32[]{:S(2)}) %all-to-all-start) | async-done | bytes 4194336 | tf_op jit(solution)/shard_map/all_to_all | solution.py:292
  119.4 5.2 %all-to-all-start.1 = ((bf16[32,2,128,256]{3,2,1,0:T(8,128)(2,1)}), bf16[32,2,128,256]{3,2,1,0:T(8,128)(2,1)}, u32[]{:S(2)}, u32[]{:S(2)}) async-start(bf16[32,2,128,256]{3,2,1,0:T(8,128)(2,1)} %pack.3), calls=%async_computation.1 | async-start | bytes 8388608 | tf_op jit(solution)/shard_map/all_to_all | solution.py:292
  124.6 0.1 fusion.8
  124.7 0.6 squeeze.39.peer_at
  125.4 0.7 squeeze.46.peer_at
  126.1 0.6 fusion.18
  126.7 1.9 pad_add_fusion.counts
  128.6 1.8 pad_add_fusion.1.counts
  130.4 0.6 slice_bitcast_fusion.8
  131.0 0.7 fusion.1
  131.7 0.1 and_select_fusion
  131.8 0.6 fusion.16
  132.5 15.9 %density.2 = (f32[2,4096]{1,0:T(2,128)}, f32[8,24,128]{2,1,0:T(8,128)}) custom-call(s32[2]{0:T(128)} %pad_add_fusion.counts, s32[49]{0:T(128)} %squeeze.39.peer_at, s32[7]{0:T(128)} %get-tuple-element.43.row_slot, s32[7]{0:T(128)} %get-tuple-element.29.col_slot, bf16[32,2,128,256]{3,2,1,0:T(8,128)(2,1)} %all-to-all-done.arrived, ...), custom_call_target="tpu_custom_call" | custom-call | flops 13153337344 | bytes 10551296 | tf_op jit(solution)/shard_map/density/pallas_call | solution.py:222
  148.4 1.0 reduce_sum.18
  149.4 69.4 %all-to-all-done.1.arrived = bf16[32,2,128,256]{3,2,1,0:T(8,128)(2,1)} async-done(((bf16[32,2,128,256]{3,2,1,0:T(8,128)(2,1)}), bf16[32,2,128,256]{3,2,1,0:T(8,128)(2,1)}, u32[]{:S(2)}, u32[]{:S(2)}) %all-to-all-start.1) | async-done | bytes 4194336 | tf_op jit(solution)/shard_map/all_to_all | solution.py:292
  218.8 11.5 %density.3 = (f32[2,4096]{1,0:T(2,128)}, f32[8,24,128]{2,1,0:T(8,128)}) custom-call(s32[2]{0:T(128)} %pad_add_fusion.1.counts, s32[49]{0:T(128)} %squeeze.46.peer_at, s32[7]{0:T(128)} %get-tuple-element.42.row_slot, s32[7]{0:T(128)} %get-tuple-element.30.col_slot, bf16[32,2,128,256]{3,2,1,0:T(8,128)(2,1)} %all-to-all-done.1.arrived, ...), custom_call_target="tpu_custom_call" | custom-call | flops 13153337344 | bytes 10551296 | tf_op jit(solution)/shard_map/density/pallas_call | solution.py:222
  230.3 1.0 reduce_sum.19
  231.3 0.7 select_maximum_fusion.mine
  232.0 19.3 %share.3 = f32[32,8,128]{2,1,0:T(8,128)} custom-call(f32[8,128]{1,0:T(8,128)} %select_maximum_fusion.mine), custom_call_target="tpu_custom_call" | custom-call | tf_op jit(solution)/shard_map/share/pallas_call | solution.py:63
  251.3 1.1 slice_bitcast_fusion.1
  252.5 0.2 copy.17
  252.7 0.7 copy.19
  253.4 0.8 pad_maximum_fusion.2
  254.2 0.7 copy.18
  (24 shorter events, 0.3 us)
Async XLA Ops:
  20.1 99.3 %all-to-all-start = ((bf16[32,2,128,256]{3,2,1,0:T(8,128)(2,1)}), bf16[32,2,128,256]{3,2,1,0:T(8,128)(2,1)}, u32[]{:S(2)}, u32[]{:S(2)}) async-start(bf16[32,2,128,256]{3,2,1,0:T(8,128)(2,1)} %pack.2), calls=%async_computation | async-start | bytes 8388608 | tf_op jit(solution)/shard_map/all_to_all | solution.py:292
  30.5 94.1 %copy-start.4 = (s32[2,7]{1,0:T(2,128)S(1)}, s32[2,7]{1,0:T(2,128)}, u32[]{:S(2)}) copy-start(s32[2,7]{1,0:T(2,128)} %param.12) | copy-start | bytes 172
  30.5 94.8 %copy-start = (f32[3,2,4096]{2,1,0:T(2,128)S(1)}, f32[3,2,4096]{2,1,0:T(2,128)}, u32[]{:S(2)}) copy-start(f32[3,2,4096]{2,1,0:T(2,128)} %param.15) | copy-start | bytes 294916
  30.5 94.9 %copy-start.1 = (f32[2,4096]{1,0:T(2,128)S(1)}, f32[2,4096]{1,0:T(2,128)}, u32[]{:S(2)}) copy-start(f32[2,4096]{1,0:T(2,128)} %param.16) | copy-start | bytes 98308
  30.5 95.6 %copy-start.5 = (s32[2]{0:T(128)S(1)}, s32[2]{0:T(128)}, u32[]{:S(2)}) copy-start(s32[2]{0:T(128)} %param.13) | copy-start | bytes 28
  30.5 95.6 %copy-start.6 = (s32[2]{0:T(128)S(1)}, s32[2]{0:T(128)}, u32[]{:S(2)}) copy-start(s32[2]{0:T(128)} %param.14) | copy-start | bytes 28
  30.5 101.2 %copy-start.2 = (s32[2,4096]{1,0:T(2,128)S(1)}, s32[2,4096]{1,0:T(2,128)}, u32[]{:S(2)}) copy-start(s32[2,4096]{1,0:T(2,128)} %param.17) | copy-start | bytes 98308
  119.4 99.4 %all-to-all-start.1 = ((bf16[32,2,128,256]{3,2,1,0:T(8,128)(2,1)}), bf16[32,2,128,256]{3,2,1,0:T(8,128)(2,1)}, u32[]{:S(2)}, u32[]{:S(2)}) async-start(bf16[32,2,128,256]{3,2,1,0:T(8,128)(2,1)} %pack.3), calls=%async_computation.1 | async-start | bytes 8388608 | tf_op jit(solution)/shard_map/all_to_all | solution.py:292
  218.8 34.6 %copy-start.3 = (f32[2,4096]{1,0:T(2,128)S(1)}, f32[2,4096]{1,0:T(2,128)}, u32[]{:S(2)}) copy-start(f32[2,4096]{1,0:T(2,128)} %get-tuple-element.6) | copy-start | bytes 98308
where the time goes:
time: 257 us; the launch traced here: 255 us
  waiting for transfers between devices  158 us (61%)
  Pallas kernels  68.9 us (27%)
  starting transfers between devices  10.2 us (4%)
  other arithmetic  9 us (4%)
  local copies, waits for them, and re-layouts  7.73 us (3%)
    all_to_all x2, waiting for transfers between devices, local(): lax.all_to_all(pack(row_at[:, b], col_at[:, b], density_first, density_se...  158 us
    pallas_call x2, Pallas kernels, share(): pl.pallas_call(functools.partial(share_kernel, row_count, col_count), out...  30.7 us
    pallas_call x2, Pallas kernels, density_of(): pl.pallas_call(functools.partial(density_kernel, run, batch), grid_spec=p...  27.5 us
    pallas_call x2, Pallas kernels, pack(): pl.pallas_call(pack_kernel, out_shape=jax.ShapeDtypeStruct(shape, first.d...  10.7 us
    all_to_all x2, starting transfers between devices, local(): lax.all_to_all(pack(row_at[:, b], col_at[:, b], density_first, density_se...  10.2 us
  transfers between devices with their start and end apart: 2, of which 2 were waited for; matrix products, arithmetic and copies ran while one was open for 3% of the time, Pallas kernels for 8%

commit v1 on v0

v1 whole, which is shorter than its diff:
```python
import functools

import jax
import jax.numpy as jnp
from jax import lax
from jax.experimental import pallas as pl
from jax.experimental.pallas import tpu as pltpu
from jax.sharding import PartitionSpec as P

TILE = 128
ATOMS = 1024
SPREAD = 8
TERMS = 9
SLOT = 16
SIGNS = (1, -1)
LEVELS = 32767.0
MESH = pl.DeviceIdType.MESH


def greet_all(me, peers, device):
    barrier = pltpu.get_barrier_semaphore()

    def greet(hop, carry):
        pl.semaphore_signal(
            barrier, inc=1, device_id=device((me + hop) % peers), device_id_type=MESH
        )
        return carry

    lax.fori_loop(1, peers, greet, 0)
    pl.semaphore_wait(barrier, peers - 1)


def fold_kernel(
    run, row_count, col_count, lists, first, second, folded, scales, starts,
    near, across, beside, behind, held, near_sem, recv_sem, send_sem, list_send, list_recv, self_sem,
):
    half = run // 2
    peers = row_count * col_count
    my_row = lax.axis_index("row")
    my_col = lax.axis_index("col")
    me = my_row * col_count + my_col
    matrices = (first, second)
    slots = near.shape[1]
    tiles = slots * row_count
    shares = [(sign * (my_col - my_row) + row_count * col_count) % col_count for sign in SIGNS]

    def device(index):
        return (index // col_count, index % col_count)

    def tile_of(d, tile_row, tile_col):
        rows = pl.ds(pl.multiple_of((tile_row // row_count) * TILE, TILE), TILE)
        cols = pl.ds(pl.multiple_of((tile_col // col_count) * TILE, TILE), TILE)
        return matrices[d].at[rows, cols]

    for d, sign in enumerate(SIGNS):

        def take(i, carry):
            mine = my_row + row_count * i
            other = (mine + sign * shares[d] + tiles) % tiles
            pltpu.make_async_copy(tile_of(d, mine, other), near.at[d, i], near_sem.at[d]).start()
            return carry

        lax.fori_loop(0, slots, take, 0)

    greet_all(me, peers, device)

    def list_copy(hop, place):
        return pltpu.make_async_remote_copy(
            src_ref=lists, dst_ref=held.at[place], send_sem=list_send.at[hop],
            recv_sem=list_recv.at[hop], device_id=device((me + hop) % peers), device_id_type=MESH,
        )

    def list_start(hop, carry):
        list_copy(hop, me).start()
        return carry

    def list_finish(hop, carry):
        list_copy(hop, (me + peers - hop) % peers).wait_recv()
        list_copy(hop, me).wait_send()
        return carry

    own_list = pltpu.make_async_copy(lists, held.at[me], self_sem)
    own_list.start()

    messages = []
    for e in range(1, half + 1):
        for d, sign in enumerate(SIGNS):
            to_row = (my_row - sign * e + 2 * row_count) % row_count
            messages.append((d, 0, e, to_row % col_count == my_col, to_row, (to_row + sign * e + col_count) % col_count))
            to_row = (my_row - sign * (e - run) + 2 * row_count) % row_count
            messages.append((d, 2, e, to_row % col_count == my_col, to_row, (to_row + sign * e + col_count) % col_count))
    for e in range(1, half + 1):
        for d, sign in enumerate(SIGNS):
            to_col = (my_col + sign * run + 2 * run * col_count) % col_count
            held_by = (sign * (to_col - my_row) + row_count * col_count) % col_count
            messages.append((d, 1, e, held_by == e, my_row, to_col))
    landings = (across, beside, behind)

    for d, kind, e, sends, to_row, to_col in messages:
        sign = SIGNS[d]
        place = (d * 3 + kind) * half + e - 1

        @pl.when(sends)
        def _():
            def send(i, carry):
                theirs = to_row + row_count * i
                shift = sign * e if kind == 0 else sign * (e - run)
                other = (theirs + shift + tiles) % tiles
                source = tile_of(d, theirs, other) if kind == 1 else tile_of(d, other, theirs)
                pltpu.make_async_remote_copy(
                    src_ref=source, dst_ref=landings[kind].at[d, i],
                    send_sem=send_sem.at[place], recv_sem=recv_sem.at[d * 3 + kind],
                    device_id=(to_row, to_col), device_id_type=MESH,
                ).start()
                return carry

            lax.fori_loop(0, slots, send, 0)

    lax.fori_loop(1, peers, list_start, 0)

    def keep(value, slot, d):
        top = jnp.maximum(jnp.max(jnp.abs(value), axis=0, keepdims=True), 1e-30)
        coded = jnp.round(value * (LEVELS / top))
        folded[slot, d] = coded.astype(jnp.int32).astype(jnp.int16)
        scales[slot, d:d + 1, :] = top * (1.0 / LEVELS)

    for d in range(2):
        pltpu.make_async_copy(near.at[d], near.at[d], near_sem.at[d]).wait()

        @pl.when(shares[d] == 0)
        def _():
            def plain(i, carry):
                keep(near[d, i].astype(jnp.float32), 2 * i, d)
                return carry

            lax.fori_loop(0, slots, plain, 0)

        @pl.when(jnp.logical_and(shares[d] >= 1, shares[d] <= half))
        def _():
            for kind in range(3):
                pltpu.make_async_copy(
                    landings[kind].at[d], landings[kind].at[d], recv_sem.at[d * 3 + kind]
                ).wait()

            def pair(i, carry):
                keep(near[d, i].astype(jnp.float32) + across[d, i].astype(jnp.float32).T, 2 * i, d)
                keep(beside[d, i].astype(jnp.float32) + behind[d, i].astype(jnp.float32).T, 2 * i + 1, d)
                return carry

            lax.fori_loop(0, slots, pair, 0)

    own_list.wait()
    lax.fori_loop(1, peers, list_finish, 0)
    lists_in = held[...]
    lane = lax.broadcasted_iota(jnp.int32, lists_in.shape, 2)
    smallest = jnp.min(jnp.where(lane < run, lists_in, tiles), axis=2, keepdims=True)
    starts[...] = jnp.broadcast_to(smallest, lists_in.shape)

    for d, kind, e, sends, to_row, to_col in messages:
        place = (d * 3 + kind) * half + e - 1

        @pl.when(sends)
        def _():
            pltpu.make_async_copy(near.at[d], near.at[d], send_sem.at[place]).wait()


def fold(lists, first, second, run, row_count, col_count):
    peers = row_count * col_count
    slots = first.shape[0] // TILE
    half = run // 2
    batches = lists.shape[0]
    band = pltpu.VMEM((2, slots, TILE, TILE), first.dtype)
    whole = pl.BlockSpec(memory_space=pltpu.VMEM)
    return pl.pallas_call(
        functools.partial(fold_kernel, run, row_count, col_count),
        out_shape=[
            jax.ShapeDtypeStruct((2 * slots, 2, TILE, TILE), jnp.int16),
            jax.ShapeDtypeStruct((2 * slots, 2, TILE), jnp.float32),
            jax.ShapeDtypeStruct((peers, batches, TILE), jnp.int32),
        ],
        in_specs=[whole, pl.BlockSpec(memory_space=pl.ANY), pl.BlockSpec(memory_space=pl.ANY)],
        out_specs=[whole] * 3,
        scratch_shapes=[
            band, band, band, band,
            pltpu.VMEM((peers, batches, TILE), jnp.int32),
            pltpu.SemaphoreType.DMA((2,)),
            pltpu.SemaphoreType.DMA((6,)),
            pltpu.SemaphoreType.DMA((6 * half,)),
            pltpu.SemaphoreType.DMA((peers,)),
            pltpu.SemaphoreType.DMA((peers,)),
            pltpu.SemaphoreType.DMA,
        ],
        compiler_params=pltpu.CompilerParams(
            collective_id=0, has_side_effects=True, vmem_limit_bytes=60 * 1024 * 1024
        ),
        name="fold",
    )(lists, first, second)


def pack_kernel(
    run, row_count, col_count, starts, place, tile_list, tile_count, folded, scales,
    out, out_scales, spots, sources, alive,
):
    slots = folded.shape[0] // 2
    half = run // 2
    batches, _, peers = out.shape[:3]
    my_row = place[0]
    my_col = place[1]

    def one(peer, carry):
        for b in range(batches):
            start = starts[peer, b, 0]
            mine = start + (my_row - start % row_count + row_count) % row_count
            slot = jnp.minimum(mine // row_count, slots - 1)
            for d, sign in enumerate(SIGNS):
                share = (sign * (my_col - my_row) + row_count * col_count) % col_count
                other = mine + sign * share
                far = jnp.logical_or(other < start, other >= start + run)
                index = 2 * slot + far.astype(jnp.int32)
                out[b, d, peer] = folded[index, d]
                out_scales[b, d, peer] = scales[index, d:d + 1, :]
        return carry

    lax.fori_loop(0, peers, one, 0)

    for b in range(batches):
        start = starts[my_row * col_count + my_col, b, 0]

        def find(j, carry):
            spots[b, tile_list[b, j] - start] = j
            return carry

        lax.fori_loop(0, run, find, 0)

        def table(k, carry):
            tile_row = (start + k) % row_count
            for d, sign in enumerate(SIGNS):
                for e in range(half + 1):
                    l = (k + sign * e + run) % run
                    tile_col = (tile_row + sign * e + col_count) % col_count
                    sources[b, d, k * (half + 1) + e] = tile_row * col_count + tile_col
                    last = jnp.maximum(spots[b, k], spots[b, l])
                    alive[b, d, k * (half + 1) + e] = jnp.where(last < tile_count[b], 1.0, 0.0)
            return carry

        lax.fori_loop(0, run, table, 0)


def pack(starts, tile_list, tile_count, folded, scales, row_count, col_count):
    run = tile_list.shape[1]
    peers, batches = starts.shape[:2]
    place = jnp.stack([lax.axis_index("row"), lax.axis_index("col")]).astype(jnp.int32)
    whole = pl.BlockSpec(memory_space=pltpu.VMEM)
    scalar = pl.BlockSpec(memory_space=pltpu.SMEM)
    return pl.pallas_call(
        functools.partial(pack_kernel, run, row_count, col_count),
        out_shape=[
            jax.ShapeDtypeStruct((batches, 2, peers, TILE, TILE), folded.dtype),
            jax.ShapeDtypeStruct((batches, 2, peers, 1, TILE), scales.dtype),
            jax.ShapeDtypeStruct((batches, run), jnp.int32),
            jax.ShapeDtypeStruct((batches, 2, run * (run // 2 + 1)), jnp.int32),
            jax.ShapeDtypeStruct((batches, 2, run * (run // 2 + 1)), jnp.float32),
        ],
        in_specs=[scalar] * 4 + [whole, whole],
        out_specs=[whole, whole, scalar, scalar, scalar],
        compiler_params=pltpu.CompilerParams(vmem_limit_bytes=60 * 1024 * 1024),
        name="pack",
    )(starts, place, tile_list, tile_count, folded, scales)


def density_kernel(
    run, row_count, col_count, spots, sources, alive, point_count, packed, packed_scales,
    basis, offsets, weights, atoms, density, every, *scratch,
):
    batches, points = weights.shape
    values, scratch = scratch[:batches], scratch[batches:]
    landed, scratch = scratch[:2 * batches], scratch[2 * batches:]
    (
        arrived_scales, blocks, sums, stage, held, basis_sem, send_sem, recv_sem, own_sem,
        scale_send, scale_recv, scale_own, last_send, last_recv, last_own,
    ) = scratch
    half = run // 2
    peers = row_count * col_count
    my_row = lax.axis_index("row")
    my_col = lax.axis_index("col")
    me = my_row * col_count + my_col
    chunk = min(512, points)
    stride = ATOMS // (peers * batches)
    pieces = [(b, d) for b in range(batches) for d in range(2)]

    def device(index):
        return (index // col_count, index % col_count)

    def load(b):
        for j in range(run):
            columns = pl.ds(j * TILE, TILE)
            pltpu.make_async_copy(basis.at[b, :, columns], values[b].at[j], basis_sem.at[b]).start()

    own = [pltpu.make_async_copy(packed.at[b, d, me], landed[b * 2 + d].at[me], own_sem.at[b * 2 + d]) for b, d in pieces]
    own_scales = pltpu.make_async_copy(packed_scales.at[:, :, me], arrived_scales.at[:, :, me], scale_own)
    own_scales.start()
    for copy in own:
        copy.start()
    greet_all(me, peers, device)

    def scale_start(hop, carry):
        to = (me + hop) % peers
        pltpu.make_async_remote_copy(
            src_ref=packed_scales.at[:, :, to], dst_ref=arrived_scales.at[:, :, me],
            send_sem=scale_send, recv_sem=scale_recv,
            device_id=device(to), device_id_type=MESH,
        ).start()
        return carry

    def start_piece(b, d):
        def send(hop, carry):
            to = (me + hop) % peers
            pltpu.make_async_remote_copy(
                src_ref=packed.at[b, d, to], dst_ref=landed[b * 2 + d].at[me],
                send_sem=send_sem.at[b * 2 + d], recv_sem=recv_sem.at[b * 2 + d],
                device_id=device(to), device_id_type=MESH,
            ).start()
            return carry

        lax.fori_loop(1, peers, send, 0)

    def wait_bytes(ref, sem):
        pltpu.make_async_copy(ref, ref, sem).wait()

    start_piece(*pieces[0])
    lax.fori_loop(1, peers, scale_start, 0)
    start_piece(*pieces[1])
    for b in range(batches):
        load(b)
    own_scales.wait()
    wait_bytes(arrived_scales.at[:, :, pl.ds(0, peers - 1)], scale_recv)
    sums[...] = jnp.zeros_like(sums)

    for index, (b, d) in enumerate(pieces):
        sign = SIGNS[d]
        own[index].wait()
        wait_bytes(landed[index].at[pl.ds(0, peers - 1)], recv_sem.at[index])
        if index + 2 < len(pieces):
            start_piece(*pieces[index + 2])
        if d == 0:
            wait_bytes(values[b], basis_sem.at[b])

        for k in range(run):
            for e in range(half + 1):
                peer = sources[b, d, k * (half + 1) + e]
                scale = arrived_scales[b, d, peer] * alive[b, d, k * (half + 1) + e]
                tile = landed[index][peer].astype(jnp.int32).astype(jnp.float32) * scale
                high = tile.astype(jnp.bfloat16)
                low = (tile - high.astype(jnp.float32)).astype(jnp.bfloat16)
                blocks[k, 0:TILE, e * TILE:(e + 1) * TILE] = high
                blocks[k, TILE:2 * TILE, e * TILE:(e + 1) * TILE] = low

        def some(c, carry):
            begin = pl.multiple_of(c * chunk, chunk)
            rows = pl.ds(begin, chunk)
            parts = [values[b][spots[b, k], rows, :] for k in range(run)]
            total = None
            for k in range(run):
                product = jnp.dot(
                    jnp.concatenate([parts[k], parts[k]], axis=1), blocks[k],
                    preferred_element_type=jnp.float32,
                )
                for e in range(half + 1):
                    part = product[:, e * TILE:(e + 1) * TILE] * parts[(k + sign * e) % run].astype(jnp.float32)
                    total = part if total is None else total + part
            row = jnp.sum(total.T, axis=0, keepdims=True)
            spot = begin + lax.broadcasted_iota(jnp.int32, (1, chunk), 1)
            row = jnp.where(spot < point_count[b], row, 0.0)
            density[d, b:b + 1, rows] = row
            x = offsets[0, b:b + 1, rows]
            y = offsets[1, b:b + 1, rows]
            z = offsets[2, b:b + 1, rows]
            w = weights[b:b + 1, rows]
            r2 = x * x + y * y + z * z
            weighted = [
                w, w * x, w * y, w * z, w * (x * y), w * (y * z),
                w * (3.0 * z * z - r2), w * (x * z), w * (x * x - y * y),
            ]
            terms = [row * item for item in weighted]
            terms += [jnp.zeros((1, chunk), jnp.float32)] * (SLOT - len(terms))
            stacked = jnp.concatenate(terms, axis=0)
            base = (me * batches + b) * stride
            atom = (atoms[b:b + 1, rows] - base + ATOMS) % ATOMS
            for j in range(SPREAD):
                chosen = jnp.where(atom == j, stacked, 0.0)
                partial = None
                for q in range(chunk // TILE):
                    part = chosen[:, q * TILE:(q + 1) * TILE]
                    partial = part if partial is None else partial + part
                at_rows = pl.ds(j * SLOT, SLOT)
                sums[index, at_rows, :] = sums[index, at_rows, :] + partial
            return carry

        lax.fori_loop(0, points // chunk, some, 0)

    for index in range(len(pieces)):
        stage[index:index + 1, :] = jnp.sum(sums[index].T, axis=0, keepdims=True)
    for index, (b, d) in enumerate(pieces):
        wait_bytes(landed[index].at[pl.ds(0, peers - 1)], send_sem.at[index])
    wait_bytes(arrived_scales.at[:, :, pl.ds(0, peers - 1)], scale_send)

    def last_start(hop, carry):
        pltpu.make_async_remote_copy(
            src_ref=stage, dst_ref=held.at[me], send_sem=last_send, recv_sem=last_recv,
            device_id=device((me + hop) % peers), device_id_type=MESH,
        ).start()
        return carry

    lax.fori_loop(1, peers, last_start, 0)
    last = pltpu.make_async_copy(stage, held.at[me], last_own)
    last.start()
    last.wait()
    wait_bytes(held.at[pl.ds(0, peers - 1)], last_recv)
    every[...] = held[...]
    wait_bytes(held.at[pl.ds(0, peers - 1)], last_send)


def density_of(
    spots, sources, alive, point_count, packed, packed_scales, basis, offsets, weights, atoms,
    row_count, col_count,
):
    batches, points, span = basis.shape
    run = span // TILE
    half = run // 2
    peers = row_count * col_count
    whole = pl.BlockSpec(memory_space=pltpu.VMEM)
    scalar = pl.BlockSpec(memory_space=pltpu.SMEM)
    anywhere = pl.BlockSpec(memory_space=pl.ANY)
    pieces = 2 * batches
    return pl.pallas_call(
        functools.partial(density_kernel, run, row_count, col_count),
        out_shape=[
            jax.ShapeDtypeStruct((2, batches, points), jnp.float32),
            jax.ShapeDtypeStruct((peers, pieces, SPREAD * SLOT), jnp.float32),
        ],
        in_specs=[scalar] * 4 + [anywhere, anywhere, anywhere, whole, whole, whole],
        out_specs=[whole, whole],
        scratch_shapes=[pltpu.VMEM((run, points, TILE), basis.dtype)] * batches
        + [pltpu.VMEM(packed.shape[2:], packed.dtype)] * pieces
        + [
            pltpu.VMEM(packed_scales.shape, packed_scales.dtype),
            pltpu.VMEM((run, 2 * TILE, (half + 1) * TILE), jnp.bfloat16),
            pltpu.VMEM((pieces, SPREAD * SLOT, TILE), jnp.float32),
            pltpu.VMEM((pieces, SPREAD * SLOT), jnp.float32),
            pltpu.VMEM((peers, pieces, SPREAD * SLOT), jnp.float32),
            pltpu.SemaphoreType.DMA((batches,)),
            pltpu.SemaphoreType.DMA((pieces,)),
            pltpu.SemaphoreType.DMA((pieces,)),
            pltpu.SemaphoreType.DMA((pieces,)),
            pltpu.SemaphoreType.DMA,
            pltpu.SemaphoreType.DMA,
            pltpu.SemaphoreType.DMA,
            pltpu.SemaphoreType.DMA,
            pltpu.SemaphoreType.DMA,
            pltpu.SemaphoreType.DMA,
        ],
        compiler_params=pltpu.CompilerParams(
            collective_id=1, has_side_effects=True, vmem_limit_bytes=62 * 1024 * 1024
        ),
        name="density",
    )(spots, sources, alive, point_count, packed, packed_scales, basis, offsets, weights, atoms)


def local(
    density_first, density_second, basis, tile_list, tile_count, point_count, offsets, weights,
    atom_of_point,
):
    row_count = lax.axis_size("row")
    col_count = lax.axis_size("col")
    peers = row_count * col_count
    batches, run = tile_list.shape
    lists = jnp.pad(tile_list, ((0, 0), (0, TILE - run)))
    folded, scales, starts = fold(lists, density_first, density_second, run, row_count, col_count)
    packed, packed_scales, spots, sources, alive = pack(
        starts, tile_list, tile_count, folded, scales, row_count, col_count
    )
    density, every = density_of(
        spots, sources, alive, point_count, packed, packed_scales, basis, offsets, weights,
        atom_of_point, row_count, col_count,
    )
    stride = ATOMS // (peers * batches)
    every = every.reshape(peers, batches, 2, SPREAD, SLOT)[..., :TERMS]
    every = every.transpose(2, 4, 0, 1, 3).reshape(2 * TERMS, peers * batches, SPREAD)
    blocks = -(-SPREAD // stride)
    every = jnp.pad(every, ((0, 0), (0, 0), (0, blocks * stride - SPREAD)))
    total = None
    for q in range(blocks):
        part = every[:, :, q * stride:(q + 1) * stride].reshape(2 * TERMS, ATOMS)
        part = jnp.roll(part, q * stride, axis=1)
        total = part if total is None else total + part
    return density, total.reshape(2, TERMS, ATOMS)


def solution(mesh):
    placed = (
        P("row", "col"),
        P("row", "col"),
        P(("row", "col"), None, None),
        P(("row", "col"), None),
        P(("row", "col")),
        P(("row", "col")),
        P(None, ("row", "col"), None),
        P(("row", "col"), None),
        P(("row", "col"), None),
    )
    return jax.shard_map(
        local,
        mesh=mesh,
        in_specs=placed,
        out_specs=(P(None, ("row", "col"), None), P()),
        check_vma=False,
    )
```

time: 257 us -> 194 us (0.75)
  waiting for transfers between devices: 158 us -> 0 us
  Pallas kernels: 68.9 us -> 187 us
  starting transfers between devices: 10.2 us -> 0 us
  other arithmetic: 9 us -> 0.59 us
  local copies, waits for them, and re-layouts: 7.73 us -> 5.08 us
    all_to_all x2 -> x0, waiting for transfers between devices: 158 us -> none  [local(): lax.all_to_all(pack(row_at[:, b], col_at[:, b], density_first, density_se...]
    pallas_call x6 -> x3, Pallas kernels: 68.9 us -> 187 us  [the longest x1 119 us: density_of(): pl.pallas_call(functools.partial(density_kernel, run, row_count, col_coun...]
    all_to_all x2 -> x0, starting transfers between devices: 10.2 us -> none  [local(): lax.all_to_all(pack(row_at[:, b], col_at[:, b], density_first, density_se...]
    another operation x4 -> x1, other arithmetic: 4.54 us -> 0.59 us  [pack(): jnp.stack([lax.axis_index('row'), lax.axis_index('col')]).astype(jnp.int32)]
  transfers between devices with their start and end apart: 2 -> 0, of which waited for: 2 -> 0; matrix products, arithmetic and copies ran while one was open for 3% -> 0% of each run, Pallas kernels for 8% -> 0%
where the time goes in v1:
time: 194 us
  Pallas kernels  187 us (96%)
  local copies, waits for them, and re-layouts  5.08 us (3%)
    pallas_call x1, Pallas kernels, density_of(): pl.pallas_call(functools.partial(density_kernel, run, row_count, col_coun...  119 us
    pallas_call x1, Pallas kernels, fold(): pl.pallas_call(functools.partial(fold_kernel, run, row_count, col_count),...  61.3 us
    pallas_call x1, Pallas kernels, pack(): pl.pallas_call(functools.partial(pack_kernel, run, row_count, col_count),...  6.43 us

profile of v1, /device:TPU:0, one launch (start us, length us, event | category | flops | bytes accessed | tf_op | source)
XLA Modules:
  0.0 193.6 jit_solution(3997708918316878434)
XLA Ops:
  0.6 0.6 pad_add_fusion.place
  1.2 1.2 pad.8.lists
  2.5 61.3 %fold.1 = (s16[24,2,128,128]{3,2,1,0:T(8,128)(2,1)}, f32[24,2,128]{2,1,0:T(2,128)}, s32[32,2,128]{2,1,0:T(2,128)}) custom-call(s32[2,128]{1,0:T(2,128)} %pad.8.lists, bf16[1536,3072]{1,0:T(8,128)(2,1)} %first.1, bf16[1536,3072]{1,0:T(8,128)(2,1)} %second.1), custom_call_target="tpu_custom_call" | custom-call | tf_op jit(solution)/shard_map/fold/pallas_call | solution.py:174
  63.8 6.4 %pack.1 = (s16[2,2,32,128,128]{4,3,2,1,0:T(8,128)(2,1)}, f32[2,2,32,1,128]{4,3,2,1,0:T(1,128)}, s32[2,7]{1,0:T(2,128)}, s32[2,2,28]{2,1,0:T(2,128)}, f32[2,2,28]{2,1,0:T(2,128)}) custom-call(s32[32,2,128]{2,1,0:T(2,128)} %get-tuple-element.12.starts, s32[2]{0:T(128)} %pad_add_fusion.place, s32[2,7]{1,0:T(2,128)} %tile_list.1, s32[2]{0:T(128)} %tile_count.1, ...), custom_call_target="tpu_custom_call" | custom-call | tf_op jit(solution)/shard_map/pack/pallas_call | solution.py:255
  70.2 119.4 %density.1 = (f32[2,2,4096]{2,1,0:T(2,128)}, f32[32,4,128]{2,1,0:T(4,128)}) custom-call(s32[2,7]{1,0:T(2,128)} %get-tuple-element.15.spots, s32[2,2,28]{2,1,0:T(2,128)} %get-tuple-element.16.sources, f32[2,2,28]{2,1,0:T(2,128)} %get-tuple-element.17.alive, s32[2]{0:T(128)} %point_count.1, s16[2,2,32,128,128]{4,3,2,1,0:T(8,128)(2,1)} %get-tuple-element.18.packed, ...), custom_call_target="tpu_custom_call" | custom-call | tf_op jit(solution)/shard_map/density/pallas_call | solution.py:435
  189.7 1.0 copy.11
  190.7 0.3 copy.16
  191.0 0.1 pad.9.clone
  191.0 0.3 reshape.17
  191.4 0.7 copy.14
  192.1 1.5 copy.19
  (1 shorter events, 0.0 us)

commit v2 on v1

v2 whole, which is shorter than its diff:
```python
import functools

import jax
import jax.numpy as jnp
from jax import lax
from jax.experimental import pallas as pl
from jax.experimental.pallas import tpu as pltpu
from jax.sharding import PartitionSpec as P

TILE = 128
ATOMS = 1024
SPREAD = 8
TERMS = 9
SLOT = 16
SIGNS = (1, -1)
LEVELS = 32767.0
MESH = pl.DeviceIdType.MESH


def greet_all(me, peers, device):
    barrier = pltpu.get_barrier_semaphore()

    def greet(hop, carry):
        pl.semaphore_signal(
            barrier, inc=1, device_id=device((me + hop) % peers), device_id_type=MESH
        )
        return carry

    lax.fori_loop(1, peers, greet, 0)
    pl.semaphore_wait(barrier, peers - 1)


def prep_kernel(run, row_count, tile_list, tile_count, lists, spots, others, alive, order):
    batches = tile_list.shape[0]
    width = run // 2 + 1
    lane = lax.broadcasted_iota(jnp.int32, lists.shape, 1)
    starts = jnp.zeros(lists.shape, jnp.int32)
    for b in range(batches):
        start = functools.reduce(jnp.minimum, [tile_list[b, j] for j in range(run)])
        starts = jnp.where(lane == b, start, starts)

        def find(j, carry):
            order[tile_list[b, j] - start] = j
            return carry

        lax.fori_loop(0, run, find, 0)

        def table(r, carry):
            offset = (r + row_count - start % row_count) % row_count
            k = jnp.minimum(offset, run - 1)
            spots[b, r] = order[k]
            for d, sign in enumerate(SIGNS):
                for e in range(width):
                    other = order[(k + sign * e + run) % run]
                    live = jnp.logical_and(offset < run, jnp.maximum(order[k], other) < tile_count[b])
                    others[b, d, r * width + e] = other
                    alive[b, d, r * width + e] = jnp.where(live, 1.0, 0.0)
            return carry

        lax.fori_loop(0, row_count, table, 0)
    lists[...] = starts


def prep(tile_list, tile_count, row_count):
    batches, run = tile_list.shape
    width = run // 2 + 1
    scalar = pl.BlockSpec(memory_space=pltpu.SMEM)
    return pl.pallas_call(
        functools.partial(prep_kernel, run, row_count),
        out_shape=[
            jax.ShapeDtypeStruct((1, TILE), jnp.int32),
            jax.ShapeDtypeStruct((batches, row_count), jnp.int32),
            jax.ShapeDtypeStruct((batches, 2, row_count * width), jnp.int32),
            jax.ShapeDtypeStruct((batches, 2, row_count * width), jnp.float32),
        ],
        in_specs=[scalar, scalar],
        out_specs=[pl.BlockSpec(memory_space=pltpu.VMEM), scalar, scalar, scalar],
        scratch_shapes=[pltpu.SMEM((run,), jnp.int32)],
        name="prep",
    )(tile_list, tile_count)


def main_kernel(
    run, row_count, col_count, spots, others, alive, point_count, lists, first, second, basis,
    offsets, weights, atoms, density, every, *scratch,
):
    batches, points = weights.shape
    pieces = [(b, d) for d in range(2) for b in range(batches)]
    values, scratch = scratch[:batches], scratch[batches:]
    outbox, scratch = scratch[:len(pieces)], scratch[len(pieces):]
    landed, scratch = scratch[:len(pieces)], scratch[len(pieces):]
    folded, fold_scales, out_scales, land_scales, scratch = (
        scratch[0:2], scratch[2:4], scratch[4:6], scratch[6:8], scratch[8:]
    )
    (
        near, across, beside, behind, held, starts, blocks, running, sums, stage, gathered,
        near_sem, fold_recv, fold_send, list_send, list_recv, list_own, basis_sem,
        send_sem, recv_sem, own_sem, scale_send, scale_recv, scale_own,
        last_send, last_recv, last_own,
    ) = scratch
    half = run // 2
    width = half + 1
    peers = row_count * col_count
    my_row = lax.axis_index("row")
    my_col = lax.axis_index("col")
    me = my_row * col_count + my_col
    matrices = (first, second)
    slots = near.shape[1]
    tiles = slots * row_count
    side = row_count // 2
    my_side = my_row // side
    chunk = min(512, points)
    stride = ATOMS // (peers * batches)
    shares = [(sign * (my_col - my_row) + row_count * col_count) % col_count for sign in SIGNS]

    def device(index):
        return (index // col_count, index % col_count)

    def wait_bytes(ref, sem):
        pltpu.make_async_copy(ref, ref, sem).wait()

    def tile_of(d, tile_row, tile_col):
        rows = pl.ds(pl.multiple_of((tile_row // row_count) * TILE, TILE), TILE)
        cols = pl.ds(pl.multiple_of((tile_col // col_count) * TILE, TILE), TILE)
        return matrices[d].at[rows, cols]

    for d, sign in enumerate(SIGNS):

        def take(i, carry):
            mine = my_row + row_count * i
            other = (mine + sign * shares[d] + tiles) % tiles
            pltpu.make_async_copy(tile_of(d, mine, other), near.at[d, i], near_sem.at[d]).start()
            return carry

        lax.fori_loop(0, slots, take, 0)

    own_list = pltpu.make_async_copy(lists, held.at[me], list_own)
    own_list.start()
    greet_all(me, peers, device)

    def list_start(hop, carry):
        pltpu.make_async_remote_copy(
            src_ref=lists, dst_ref=held.at[me], send_sem=list_send, recv_sem=list_recv,
            device_id=device((me + hop) % peers), device_id_type=MESH,
        ).start()
        return carry

    lax.fori_loop(1, peers, list_start, 0)

    messages = []
    for d, sign in enumerate(SIGNS):
        for e in range(1, half + 1):
            for kind, shift in ((0, sign * e), (2, sign * (e - run))):
                to_row = (my_row - shift + 2 * row_count) % row_count
                to_col = (to_row + sign * e + col_count) % col_count
                messages.append((d, kind, e, to_row % col_count == my_col, to_row, to_col))
        for e in range(1, half + 1):
            to_col = (my_col + sign * run + 2 * run * col_count) % col_count
            share = (sign * (to_col - my_row) + row_count * col_count) % col_count
            messages.append((d, 1, e, share == e, my_row, to_col))
    landings = (across, beside, behind)

    for d, kind, e, sends, to_row, to_col in messages:
        sign = SIGNS[d]
        place = (d * 3 + kind) * half + e - 1

        @pl.when(sends)
        def _():
            def send(i, carry):
                theirs = to_row + row_count * i
                shift = sign * e if kind == 0 else sign * (e - run)
                other = (theirs + shift + tiles) % tiles
                source = tile_of(d, theirs, other) if kind == 1 else tile_of(d, other, theirs)
                pltpu.make_async_remote_copy(
                    src_ref=source, dst_ref=landings[kind].at[d, i],
                    send_sem=fold_send.at[place], recv_sem=fold_recv.at[d * 3 + kind],
                    device_id=(to_row, to_col), device_id_type=MESH,
                ).start()
                return carry

            lax.fori_loop(0, slots, send, 0)

    for b in range(batches):
        for j in range(run):
            columns = pl.ds(j * TILE, TILE)
            pltpu.make_async_copy(basis.at[b, :, columns], values[b].at[j], basis_sem.at[b]).start()

    own_list.wait()
    wait_bytes(held.at[pl.ds(0, peers - 1)], list_recv)
    to_scalars = pltpu.make_async_copy(held, starts, list_own)
    to_scalars.start()
    to_scalars.wait()

    def keep(value, d, slot):
        top = jnp.maximum(jnp.max(jnp.abs(value), axis=0, keepdims=True), 1e-30)
        folded[d][slot] = jnp.round(value * (LEVELS / top)).astype(jnp.int32).astype(jnp.int16)
        fold_scales[d][slot] = top * (1.0 / LEVELS)

    def fold(d):
        wait_bytes(near.at[d], near_sem.at[d])

        @pl.when(shares[d] == 0)
        def _():
            def plain(i, carry):
                value = near[d, i].astype(jnp.float32)
                keep(value, d, 2 * i)
                keep(value, d, 2 * i + 1)
                return carry

            lax.fori_loop(0, slots, plain, 0)

        @pl.when(jnp.logical_and(shares[d] >= 1, shares[d] <= half))
        def _():
            for kind in range(3):
                wait_bytes(landings[kind].at[d], fold_recv.at[d * 3 + kind])

            def pair(i, carry):
                keep(near[d, i].astype(jnp.float32) + across[d, i].astype(jnp.float32).T, d, 2 * i)
                keep(beside[d, i].astype(jnp.float32) + behind[d, i].astype(jnp.float32).T, d, 2 * i + 1)
                return carry

            lax.fori_loop(0, slots, pair, 0)

        if col_count > width:

            @pl.when(shares[d] > half)
            def _():
                folded[d][...] = jnp.zeros_like(folded[d])
                fold_scales[d][...] = jnp.zeros_like(fold_scales[d])

    def pack(d):
        sign = SIGNS[d]

        def one(peer, carry):
            for b in range(batches):
                start = starts[peer, 0, b]
                mine = start + (my_row + row_count - start % row_count) % row_count
                slot = jnp.minimum(mine // row_count, slots - 1)
                other = mine + sign * shares[d]
                inside = jnp.logical_and(other >= start, other < start + run)
                index = 2 * slot + jnp.where(inside, 0, 1)
                outbox[d * batches + b][peer] = folded[d][index]
                out_scales[d][peer, b:b + 1, :] = fold_scales[d][index]
            return carry

        lax.fori_loop(0, peers, one, 0)

    def send_scales(d):
        pltpu.make_async_copy(out_scales[d].at[me], land_scales[d].at[me], scale_own.at[d]).start()

        def send(hop, carry):
            to = (me + hop) % peers
            pltpu.make_async_remote_copy(
                src_ref=out_scales[d].at[to], dst_ref=land_scales[d].at[me],
                send_sem=scale_send.at[d], recv_sem=scale_recv.at[d],
                device_id=device(to), device_id_type=MESH,
            ).start()
            return carry

        lax.fori_loop(1, peers, send, 0)

    def send_piece(index):
        pltpu.make_async_copy(outbox[index].at[me], landed[index].at[me], own_sem.at[index]).start()

        def send(hop, carry):
            to = (me + hop) % peers
            far = ((to // col_count) // side + my_side) % 2
            pltpu.make_async_remote_copy(
                src_ref=outbox[index].at[to], dst_ref=landed[index].at[me],
                send_sem=send_sem.at[index], recv_sem=recv_sem.at[index * 2 + far],
                device_id=device(to), device_id_type=MESH,
            ).start()
            return carry

        lax.fori_loop(1, peers, send, 0)

    def compute(index, far):
        b, d = pieces[index]
        sign = SIGNS[d]
        low_row = ((my_side + far) % 2) * side

        for i in range(side):
            for e in range(width):
                row = low_row + i
                peer = row * col_count + (row + sign * e + col_count) % col_count
                scale = land_scales[d][peer, b:b + 1, :] * alive[b, d, row * width + e]
                tile = landed[index][peer].astype(jnp.int32).astype(jnp.float32) * scale
                high = tile.astype(jnp.bfloat16)
                low = (tile - high.astype(jnp.float32)).astype(jnp.bfloat16)
                blocks[i, 0:TILE, e * TILE:(e + 1) * TILE] = high
                blocks[i, TILE:2 * TILE, e * TILE:(e + 1) * TILE] = low

        def some(c, carry):
            begin = pl.multiple_of(c * chunk, chunk)
            rows = pl.ds(begin, chunk)
            total = running[rows, :] if far else None
            for i in range(side):
                row = low_row + i
                part = values[b][spots[b, row], rows, :]
                product = jnp.dot(
                    jnp.concatenate([part, part], axis=1), blocks[i],
                    preferred_element_type=jnp.float32,
                )
                for e in range(width):
                    other = values[b][others[b, d, row * width + e], rows, :] if e else part
                    term = product[:, e * TILE:(e + 1) * TILE] * other.astype(jnp.float32)
                    total = term if total is None else total + term
            if not far:
                running[rows, :] = total
                return carry
            line = jnp.sum(total.T, axis=0, keepdims=True)
            spot = begin + lax.broadcasted_iota(jnp.int32, (1, chunk), 1)
            line = jnp.where(spot < point_count[b], line, 0.0)
            density[d, b:b + 1, rows] = line
            x = offsets[0, b:b + 1, rows]
            y = offsets[1, b:b + 1, rows]
            z = offsets[2, b:b + 1, rows]
            w = weights[b:b + 1, rows]
            r2 = x * x + y * y + z * z
            weighted = [
                w, w * x, w * y, w * z, w * (x * y), w * (y * z),
                w * (3.0 * z * z - r2), w * (x * z), w * (x * x - y * y),
            ]
            terms = [line * item for item in weighted]
            terms += [jnp.zeros((1, chunk), jnp.float32)] * (SLOT - len(terms))
            stacked = jnp.concatenate(terms, axis=0)
            base = (me * batches + b) * stride
            atom = (atoms[b:b + 1, rows] - base + ATOMS) % ATOMS
            for j in range(SPREAD):
                chosen = jnp.where(atom == j, stacked, 0.0)
                partial = None
                for q in range(chunk // TILE):
                    part = chosen[:, q * TILE:(q + 1) * TILE]
                    partial = part if partial is None else partial + part
                at_rows = pl.ds(j * SLOT, SLOT)
                sums[index, at_rows, :] = sums[index, at_rows, :] + partial
            return carry

        lax.fori_loop(0, points // chunk, some, 0)

    sums[...] = jnp.zeros_like(sums)
    for d in range(2):
        fold(d)
        pack(d)
        send_scales(d)
        if d == 0:
            for b in range(batches):
                send_piece(b)

    for b in range(batches):
        wait_bytes(values[b], basis_sem.at[b])
    for index, (b, d) in enumerate(pieces):
        if b == 0:
            pltpu.make_async_copy(out_scales[d].at[me], land_scales[d].at[me], scale_own.at[d]).wait()
            wait_bytes(land_scales[d].at[pl.ds(0, peers - 1)], scale_recv.at[d])
        pltpu.make_async_copy(outbox[index].at[me], landed[index].at[me], own_sem.at[index]).wait()
        wait_bytes(landed[index].at[pl.ds(0, peers // 2 - 1)], recv_sem.at[index * 2])
        if index + batches < len(pieces):
            send_piece(index + batches)
        compute(index, 0)
        wait_bytes(landed[index].at[pl.ds(0, peers // 2)], recv_sem.at[index * 2 + 1])
        compute(index, 1)

    for index in range(len(pieces)):
        stage[index:index + 1, :] = jnp.sum(sums[index].T, axis=0, keepdims=True)
    for index in range(len(pieces)):
        wait_bytes(landed[index].at[pl.ds(0, peers - 1)], send_sem.at[index])
    for d in range(2):
        wait_bytes(land_scales[d].at[pl.ds(0, peers - 1)], scale_send.at[d])
    wait_bytes(held.at[pl.ds(0, peers - 1)], list_send)

    def last_start(hop, carry):
        pltpu.make_async_remote_copy(
            src_ref=stage, dst_ref=gathered.at[me], send_sem=last_send, recv_sem=last_recv,
            device_id=device((me + hop) % peers), device_id_type=MESH,
        ).start()
        return carry

    lax.fori_loop(1, peers, last_start, 0)
    last = pltpu.make_async_copy(stage, gathered.at[me], last_own)
    last.start()
    for d, kind, e, sends, to_row, to_col in messages:
        place = (d * 3 + kind) * half + e - 1

        @pl.when(sends)
        def _():
            wait_bytes(near.at[d], fold_send.at[place])

    last.wait()
    wait_bytes(gathered.at[pl.ds(0, peers - 1)], last_recv)
    every[...] = gathered[...]
    wait_bytes(gathered.at[pl.ds(0, peers - 1)], last_send)


def density_of(
    spots, others, alive, point_count, lists, first, second, basis, offsets, weights, atoms,
    row_count, col_count,
):
    batches, points, span = basis.shape
    run = span // TILE
    half = run // 2
    peers = row_count * col_count
    slots = first.shape[0] // TILE
    pieces = 2 * batches
    whole = pl.BlockSpec(memory_space=pltpu.VMEM)
    scalar = pl.BlockSpec(memory_space=pltpu.SMEM)
    anywhere = pl.BlockSpec(memory_space=pl.ANY)
    copies = pltpu.SemaphoreType.DMA
    return pl.pallas_call(
        functools.partial(main_kernel, run, row_count, col_count),
        out_shape=[
            jax.ShapeDtypeStruct((2, batches, points), jnp.float32),
            jax.ShapeDtypeStruct((peers, pieces, SPREAD * SLOT), jnp.float32),
        ],
        in_specs=[scalar] * 4 + [whole] + [anywhere] * 3 + [whole] * 3,
        out_specs=[whole, whole],
        scratch_shapes=[pltpu.VMEM((run, points, TILE), basis.dtype)] * batches
        + [pltpu.VMEM((peers, TILE, TILE), jnp.int16)] * (2 * pieces)
        + [pltpu.VMEM((2 * slots, TILE, TILE), jnp.int16)] * 2
        + [pltpu.VMEM((2 * slots, 1, TILE), jnp.float32)] * 2
        + [pltpu.VMEM((peers, batches, TILE), jnp.float32)] * 4
        + [pltpu.VMEM((2, slots, TILE, TILE), first.dtype)] * 4
        + [
            pltpu.VMEM((peers, 1, TILE), jnp.int32),
            pltpu.SMEM((peers, 1, TILE), jnp.int32),
            pltpu.VMEM((row_count // 2, 2 * TILE, (half + 1) * TILE), jnp.bfloat16),
            pltpu.VMEM((points, TILE), jnp.float32),
            pltpu.VMEM((pieces, SPREAD * SLOT, TILE), jnp.float32),
            pltpu.VMEM((pieces, SPREAD * SLOT), jnp.float32),
            pltpu.VMEM((peers, pieces, SPREAD * SLOT), jnp.float32),
            copies((2,)), copies((6,)), copies((6 * half,)), copies, copies, copies,
            copies((batches,)), copies((pieces,)), copies((2 * pieces,)), copies((pieces,)),
            copies((2,)), copies((2,)), copies((2,)), copies, copies, copies,
        ],
        compiler_params=pltpu.CompilerParams(
            collective_id=0, has_side_effects=True, vmem_limit_bytes=62 * 1024 * 1024
        ),
        name="density",
    )(spots, others, alive, point_count, lists, first, second, basis, offsets, weights, atoms)


def local(
    density_first, density_second, basis, tile_list, tile_count, point_count, offsets, weights,
    atom_of_point,
):
    row_count = lax.axis_size("row")
    col_count = lax.axis_size("col")
    peers = row_count * col_count
    batches = tile_list.shape[0]
    lists, spots, others, alive = prep(tile_list, tile_count, row_count)
    density, every = density_of(
        spots, others, alive, point_count, lists, density_first, density_second, basis, offsets,
        weights, atom_of_point, row_count, col_count,
    )
    stride = ATOMS // (peers * batches)
    every = every.reshape(peers, 2, batches, SPREAD, SLOT)[..., :TERMS]
    every = every.transpose(1, 4, 0, 2, 3).reshape(2 * TERMS, peers * batches, SPREAD)
    blocks = -(-SPREAD // stride)
    every = jnp.pad(every, ((0, 0), (0, 0), (0, blocks * stride - SPREAD)))
    total = None
    for q in range(blocks):
        part = every[:, :, q * stride:(q + 1) * stride].reshape(2 * TERMS, ATOMS)
        part = jnp.roll(part, q * stride, axis=1)
        total = part if total is None else total + part
    return density, total.reshape(2, TERMS, ATOMS)


def solution(mesh):
    placed = (
        P("row", "col"),
        P("row", "col"),
        P(("row", "col"), None, None),
        P(("row", "col"), None),
        P(("row", "col")),
        P(("row", "col")),
        P(None, ("row", "col"), None),
        P(("row", "col"), None),
        P(("row", "col"), None),
    )
    return jax.shard_map(
        local,
        mesh=mesh,
        in_specs=placed,
        out_specs=(P(None, ("row", "col"), None), P()),
        check_vma=False,
    )
```

time: 194 us -> 177 us (0.912)
  Pallas kernels: 187 us -> 172 us
    pallas_call x3 -> x2, Pallas kernels: 187 us -> 172 us  [the longest x1 170 us: density_of(): pl.pallas_call(functools.partial(main_kernel, run, row_count, col_count),...]
where the time goes in v2:
time: 177 us
  Pallas kernels  172 us (97%)
  local copies, waits for them, and re-layouts  3.84 us (2%)
    pallas_call x1, Pallas kernels, density_of(): pl.pallas_call(functools.partial(main_kernel, run, row_count, col_count),...  170 us

profile of v2, /device:TPU:0, one launch (start us, length us, event | category | flops | bytes accessed | tf_op | source)
XLA Modules:
  0.0 176.7 jit_solution(7450752690024301562)
XLA Ops:
  0.6 2.5 %prep.1 = (s32[1,128]{1,0:T(1,128)}, s32[2,8]{1,0:T(2,128)}, s32[2,2,32]{2,1,0:T(2,128)}, f32[2,2,32]{2,1,0:T(2,128)}) custom-call(s32[2,7]{1,0:T(2,128)} %tile_list.1, s32[2]{0:T(128)} %tile_count.1), custom_call_target="tpu_custom_call" | custom-call | tf_op jit(solution)/shard_map/prep/pallas_call | solution.py:68
  3.2 169.7 %density.1 = (f32[2,2,4096]{2,1,0:T(2,128)}, f32[32,4,128]{2,1,0:T(4,128)}) custom-call(s32[2,8]{1,0:T(2,128)} %get-tuple-element.8.spots, s32[2,2,32]{2,1,0:T(2,128)} %get-tuple-element.9.others, f32[2,2,32]{2,1,0:T(2,128)} %get-tuple-element.10.alive, s32[2]{0:T(128)} %point_count.1, s32[1,128]{1,0:T(1,128)} %get-tuple-element.11.lists, ...), custom_call_target="tpu_custom_call" | custom-call | tf_op jit(solution)/shard_map/density/pallas_call | solution.py:409
  172.9 1.0 copy.11
  173.8 0.3 copy.16
  174.2 0.1 pad.4.clone
  174.2 0.3 reshape.17
  174.6 0.7 copy.14
  175.2 1.5 copy.19
  (1 shorter events, 0.0 us)

commit v3 on v2

--- a/solution.py
+++ b/solution.py
@@ -30,58 +30,8 @@
     pl.semaphore_wait(barrier, peers - 1)
 
 
-def prep_kernel(run, row_count, tile_list, tile_count, lists, spots, others, alive, order):
-    batches = tile_list.shape[0]
-    width = run // 2 + 1
-    lane = lax.broadcasted_iota(jnp.int32, lists.shape, 1)
-    starts = jnp.zeros(lists.shape, jnp.int32)
-    for b in range(batches):
-        start = functools.reduce(jnp.minimum, [tile_list[b, j] for j in range(run)])
-        starts = jnp.where(lane == b, start, starts)
-
-        def find(j, carry):
-            order[tile_list[b, j] - start] = j
-            return carry
-
-        lax.fori_loop(0, run, find, 0)
-
-        def table(r, carry):
-            offset = (r + row_count - start % row_count) % row_count
-            k = jnp.minimum(offset, run - 1)
-            spots[b, r] = order[k]
-            for d, sign in enumerate(SIGNS):
-                for e in range(width):
-                    other = order[(k + sign * e + run) % run]
-                    live = jnp.logical_and(offset < run, jnp.maximum(order[k], other) < tile_count[b])
-                    others[b, d, r * width + e] = other
-                    alive[b, d, r * width + e] = jnp.where(live, 1.0, 0.0)
-            return carry
-
-        lax.fori_loop(0, row_count, table, 0)
-    lists[...] = starts
-
-
-def prep(tile_list, tile_count, row_count):
-    batches, run = tile_list.shape
-    width = run // 2 + 1
-    scalar = pl.BlockSpec(memory_space=pltpu.SMEM)
-    return pl.pallas_call(
-        functools.partial(prep_kernel, run, row_count),
-        out_shape=[
-            jax.ShapeDtypeStruct((1, TILE), jnp.int32),
-            jax.ShapeDtypeStruct((batches, row_count), jnp.int32),
-            jax.ShapeDtypeStruct((batches, 2, row_count * width), jnp.int32),
-            jax.ShapeDtypeStruct((batches, 2, row_count * width), jnp.float32),
-        ],
-        in_specs=[scalar, scalar],
-        out_specs=[pl.BlockSpec(memory_space=pltpu.VMEM), scalar, scalar, scalar],
-        scratch_shapes=[pltpu.SMEM((run,), jnp.int32)],
-        name="prep",
-    )(tile_list, tile_count)
-
-
 def main_kernel(
-    run, row_count, col_count, spots, others, alive, point_count, lists, first, second, basis,
+    run, row_count, col_count, tile_list, tile_count, point_count, first, second, basis,
     offsets, weights, atoms, density, every, *scratch,
 ):
     batches, points = weights.shape
@@ -93,7 +43,8 @@
         scratch[0:2], scratch[2:4], scratch[4:6], scratch[6:8], scratch[8:]
     )
     (
-        near, across, beside, behind, held, starts, blocks, running, sums, stage, gathered,
+        sources, alive, order, lists, fold_out, gather_sem,
+        near, across, beside, behind, held, starts, blocks, sums, stage, gathered,
         near_sem, fold_recv, fold_send, list_send, list_recv, list_own, basis_sem,
         send_sem, recv_sem, own_sem, scale_send, scale_recv, scale_own,
         last_send, last_recv, last_own,
@@ -107,8 +58,6 @@
     matrices = (first, second)
     slots = near.shape[1]
     tiles = slots * row_count
-    side = row_count // 2
-    my_side = my_row // side
     chunk = min(512, points)
     stride = ATOMS // (peers * batches)
     shares = [(sign * (my_col - my_row) + row_count * col_count) % col_count for sign in SIGNS]
@@ -134,18 +83,13 @@
 
         lax.fori_loop(0, slots, take, 0)
 
-    own_list = pltpu.make_async_copy(lists, held.at[me], list_own)
-    own_list.start()
-    greet_all(me, peers, device)
-
-    def list_start(hop, carry):
-        pltpu.make_async_remote_copy(
-            src_ref=lists, dst_ref=held.at[me], send_sem=list_send, recv_sem=list_recv,
-            device_id=device((me + hop) % peers), device_id_type=MESH,
-        ).start()
-        return carry
-
-    lax.fori_loop(1, peers, list_start, 0)
+    lane = lax.broadcasted_iota(jnp.int32, lists.shape, 1)
+    firsts = jnp.zeros(lists.shape, jnp.int32)
+    begins = []
+    for b in range(batches):
+        begins.append(functools.reduce(jnp.minimum, [tile_list[b, j] for j in range(run)]))
+        firsts = jnp.where(lane == b, begins[b], firsts)
+    lists[...] = firsts
 
     messages = []
     for d, sign in enumerate(SIGNS):
@@ -166,24 +110,66 @@
 
         @pl.when(sends)
         def _():
-            def send(i, carry):
+            def gather(i, carry):
                 theirs = to_row + row_count * i
                 shift = sign * e if kind == 0 else sign * (e - run)
                 other = (theirs + shift + tiles) % tiles
                 source = tile_of(d, theirs, other) if kind == 1 else tile_of(d, other, theirs)
-                pltpu.make_async_remote_copy(
-                    src_ref=source, dst_ref=landings[kind].at[d, i],
-                    send_sem=fold_send.at[place], recv_sem=fold_recv.at[d * 3 + kind],
-                    device_id=(to_row, to_col), device_id_type=MESH,
-                ).start()
+                pltpu.make_async_copy(source, fold_out.at[place, i], gather_sem.at[place]).start()
                 return carry
 
-            lax.fori_loop(0, slots, send, 0)
+            lax.fori_loop(0, slots, gather, 0)
+
+    greet_all(me, peers, device)
+    own_list = pltpu.make_async_copy(lists, held.at[me], list_own)
+    own_list.start()
+
+    def list_start(hop, carry):
+        pltpu.make_async_remote_copy(
+            src_ref=lists, dst_ref=held.at[me], send_sem=list_send, recv_sem=list_recv,
+            device_id=device((me + hop) % peers), device_id_type=MESH,
+        ).start()
+        return carry
+
+    lax.fori_loop(1, peers, list_start, 0)
+
+    for d, kind, e, sends, to_row, to_col in messages:
+        place = (d * 3 + kind) * half + e - 1
+
+        @pl.when(sends)
+        def _():
+            wait_bytes(fold_out.at[place], gather_sem.at[place])
+            pltpu.make_async_remote_copy(
+                src_ref=fold_out.at[place], dst_ref=landings[kind].at[d],
+                send_sem=fold_send.at[place], recv_sem=fold_recv.at[d * 3 + kind],
+                device_id=(to_row, to_col), device_id_type=MESH,
+            ).start()
 
     for b in range(batches):
         for j in range(run):
             columns = pl.ds(j * TILE, TILE)
             pltpu.make_async_copy(basis.at[b, :, columns], values[b].at[j], basis_sem.at[b]).start()
+
+    for b in range(batches):
+        start = begins[b]
+        for k in range(run):
+            spot = 0
+            for j in range(1, run):
+                spot = jnp.maximum(spot, jnp.where(tile_list[b, j] == start + k, j, 0))
+            order[b, k] = spot
+
+        def table(l, carry):
+            for d, sign in enumerate(SIGNS):
+                for e in range(width):
+                    k = (l - sign * e + run) % run
+                    tile_row = (start + k) % row_count
+                    tile_col = (tile_row + sign * e + col_count) % col_count
+                    last = jnp.maximum(order[b, k], order[b, l])
+                    sources[b, d, l * width + e] = tile_row * col_count + tile_col
+                    alive[b, d, l * width + e] = jnp.where(last < tile_count[b], 1.0, 0.0)
+            return carry
+
+        lax.fori_loop(0, run, table, 0)
 
     own_list.wait()
     wait_bytes(held.at[pl.ds(0, peers - 1)], list_recv)
@@ -263,51 +249,42 @@
         pltpu.make_async_copy(outbox[index].at[me], landed[index].at[me], own_sem.at[index]).start()
 
         def send(hop, carry):
-            to = (me + hop) % peers
-            far = ((to // col_count) // side + my_side) % 2
+            to = (me + peers // 2 + hop - 1 + hop // (peers // 2 + 1)) % peers
             pltpu.make_async_remote_copy(
                 src_ref=outbox[index].at[to], dst_ref=landed[index].at[me],
-                send_sem=send_sem.at[index], recv_sem=recv_sem.at[index * 2 + far],
+                send_sem=send_sem.at[index], recv_sem=recv_sem.at[index],
                 device_id=device(to), device_id_type=MESH,
             ).start()
             return carry
 
         lax.fori_loop(1, peers, send, 0)
 
-    def compute(index, far):
+    def compute(index):
         b, d = pieces[index]
         sign = SIGNS[d]
-        low_row = ((my_side + far) % 2) * side
-
-        for i in range(side):
+
+        for l in range(run):
             for e in range(width):
-                row = low_row + i
-                peer = row * col_count + (row + sign * e + col_count) % col_count
-                scale = land_scales[d][peer, b:b + 1, :] * alive[b, d, row * width + e]
+                peer = sources[b, d, l * width + e]
+                scale = land_scales[d][peer, b:b + 1, :] * alive[b, d, l * width + e]
                 tile = landed[index][peer].astype(jnp.int32).astype(jnp.float32) * scale
                 high = tile.astype(jnp.bfloat16)
                 low = (tile - high.astype(jnp.float32)).astype(jnp.bfloat16)
-                blocks[i, 0:TILE, e * TILE:(e + 1) * TILE] = high
-                blocks[i, TILE:2 * TILE, e * TILE:(e + 1) * TILE] = low
+                blocks[l, e * TILE:(e + 1) * TILE, 0:TILE] = high
+                blocks[l, e * TILE:(e + 1) * TILE, TILE:2 * TILE] = low
 
         def some(c, carry):
             begin = pl.multiple_of(c * chunk, chunk)
             rows = pl.ds(begin, chunk)
-            total = running[rows, :] if far else None
-            for i in range(side):
-                row = low_row + i
-                part = values[b][spots[b, row], rows, :]
+            parts = [values[b][order[b, k], rows, :] for k in range(run)]
+            total = None
+            for l in range(run):
                 product = jnp.dot(
-                    jnp.concatenate([part, part], axis=1), blocks[i],
-                    preferred_element_type=jnp.float32,
+                    jnp.concatenate([parts[(l - sign * e) % run] for e in range(width)], axis=1),
+                    blocks[l], preferred_element_type=jnp.float32,
                 )
-                for e in range(width):
-                    other = values[b][others[b, d, row * width + e], rows, :] if e else part
-                    term = product[:, e * TILE:(e + 1) * TILE] * other.astype(jnp.float32)
-                    total = term if total is None else total + term
-            if not far:
-                running[rows, :] = total
-                return carry
+                term = (product[:, 0:TILE] + product[:, TILE:2 * TILE]) * parts[l].astype(jnp.float32)
+                total = term if total is None else total + term
             line = jnp.sum(total.T, axis=0, keepdims=True)
             spot = begin + lax.broadcasted_iota(jnp.int32, (1, chunk), 1)
             line = jnp.where(spot < point_count[b], line, 0.0)
@@ -343,9 +320,8 @@
         fold(d)
         pack(d)
         send_scales(d)
-        if d == 0:
-            for b in range(batches):
-                send_piece(b)
+        for b in range(batches):
+            send_piece(d * batches + b)
 
     for b in range(batches):
         wait_bytes(values[b], basis_sem.at[b])
@@ -354,12 +330,8 @@
             pltpu.make_async_copy(out_scales[d].at[me], land_scales[d].at[me], scale_own.at[d]).wait()
             wait_bytes(land_scales[d].at[pl.ds(0, peers - 1)], scale_recv.at[d])
         pltpu.make_async_copy(outbox[index].at[me], landed[index].at[me], own_sem.at[index]).wait()
-        wait_bytes(landed[index].at[pl.ds(0, peers // 2 - 1)], recv_sem.at[index * 2])
-        if index + batches < len(pieces):
-            send_piece(index + batches)
-        compute(index, 0)
-        wait_bytes(landed[index].at[pl.ds(0, peers // 2)], recv_sem.at[index * 2 + 1])
-        compute(index, 1)
+        wait_bytes(landed[index].at[pl.ds(0, peers - 1)], recv_sem.at[index])
+        compute(index)
 
     for index in range(len(pieces)):
         stage[index:index + 1, :] = jnp.sum(sums[index].T, axis=0, keepdims=True)
@@ -393,7 +365,7 @@
 
 
 def density_of(
-    spots, others, alive, point_count, lists, first, second, basis, offsets, weights, atoms,
+    tile_list, tile_count, point_count, first, second, basis, offsets, weights, atoms,
     row_count, col_count,
 ):
     batches, points, span = basis.shape
@@ -412,31 +384,38 @@
             jax.ShapeDtypeStruct((2, batches, points), jnp.float32),
             jax.ShapeDtypeStruct((peers, pieces, SPREAD * SLOT), jnp.float32),
         ],
-        in_specs=[scalar] * 4 + [whole] + [anywhere] * 3 + [whole] * 3,
+        in_specs=[scalar] * 3 + [anywhere] * 3 + [whole] * 3,
         out_specs=[whole, whole],
         scratch_shapes=[pltpu.VMEM((run, points, TILE), basis.dtype)] * batches
         + [pltpu.VMEM((peers, TILE, TILE), jnp.int16)] * (2 * pieces)
         + [pltpu.VMEM((2 * slots, TILE, TILE), jnp.int16)] * 2
         + [pltpu.VMEM((2 * slots, 1, TILE), jnp.float32)] * 2
         + [pltpu.VMEM((peers, batches, TILE), jnp.float32)] * 4
+        + [
+            pltpu.SMEM((batches, 2, run * (half + 1)), jnp.int32),
+            pltpu.SMEM((batches, 2, run * (half + 1)), jnp.float32),
+            pltpu.SMEM((batches, run), jnp.int32),
+            pltpu.VMEM((1, TILE), jnp.int32),
+            pltpu.VMEM((6 * half, slots, TILE, TILE), first.dtype),
+            copies((6 * half,)),
+        ]
         + [pltpu.VMEM((2, slots, TILE, TILE), first.dtype)] * 4
         + [
             pltpu.VMEM((peers, 1, TILE), jnp.int32),
             pltpu.SMEM((peers, 1, TILE), jnp.int32),
-            pltpu.VMEM((row_count // 2, 2 * TILE, (half + 1) * TILE), jnp.bfloat16),
-            pltpu.VMEM((points, TILE), jnp.float32),
+            pltpu.VMEM((run, (half + 1) * TILE, 2 * TILE), jnp.bfloat16),
             pltpu.VMEM((pieces, SPREAD * SLOT, TILE), jnp.float32),
             pltpu.VMEM((pieces, SPREAD * SLOT), jnp.float32),
             pltpu.VMEM((peers, pieces, SPREAD * SLOT), jnp.float32),
             copies((2,)), copies((6,)), copies((6 * half,)), copies, copies, copies,
-            copies((batches,)), copies((pieces,)), copies((2 * pieces,)), copies((pieces,)),
+            copies((batches,)), copies((pieces,)), copies((pieces,)), copies((pieces,)),
             copies((2,)), copies((2,)), copies((2,)), copies, copies, copies,
         ],
         compiler_params=pltpu.CompilerParams(
             collective_id=0, has_side_effects=True, vmem_limit_bytes=62 * 1024 * 1024
         ),
         name="density",
-    )(spots, others, alive, point_count, lists, first, second, basis, offsets, weights, atoms)
+    )(tile_list, tile_count, point_count, first, second, basis, offsets, weights, atoms)
 
 
 def local(
@@ -447,9 +426,8 @@
     col_count = lax.axis_size("col")
     peers = row_count * col_count
     batches = tile_list.shape[0]
-    lists, spots, others, alive = prep(tile_list, tile_count, row_count)
     density, every = density_of(
-        spots, others, alive, point_count, lists, density_first, density_second, basis, offsets,
+        tile_list, tile_count, point_count, density_first, density_second, basis, offsets,
         weights, atom_of_point, row_count, col_count,
     )
     stride = ATOMS // (peers * batches)

time: 177 us -> 169 us (0.955)
  Pallas kernels: 172 us -> 164 us
    pallas_call x1, Pallas kernels: 170 us -> 164 us  [density_of(): pl.pallas_call(functools.partial(main_kernel, run, row_count, col_count),...]
    pallas_call x1 -> x0, Pallas kernels: 2.52 us -> none  [prep(): pl.pallas_call(functools.partial(prep_kernel, run, row_count), out_shape=...]
where the time goes in v3:
time: 169 us
  Pallas kernels  164 us (97%)
  local copies, waits for them, and re-layouts  3.84 us (2%)
    pallas_call x1, Pallas kernels, density_of(): pl.pallas_call(functools.partial(main_kernel, run, row_count, col_count),...  164 us

profile of v3, /device:TPU:0, one launch (start us, length us, event | category | flops | bytes accessed | tf_op | source)
XLA Modules:
  0.0 168.7 jit_solution(17153968486349415597)
XLA Ops:
  0.6 164.2 %density.1 = (f32[2,2,4096]{2,1,0:T(2,128)}, f32[32,4,128]{2,1,0:T(4,128)}) custom-call(s32[2,7]{1,0:T(2,128)} %tile_list.1, s32[2]{0:T(128)} %tile_count.1, s32[2]{0:T(128)} %point_count.1, bf16[1536,3072]{1,0:T(8,128)(2,1)} %first.1, bf16[1536,3072]{1,0:T(8,128)(2,1)} %second.1, bf16[2,4096,896]{2,1,0:T(8,128)(2,1)} %basis.1, f32[3,2,4096]{2,1,0:T(2,128)} %offsets.1, ...), custom_call_target="tpu_custom_call" | custom-call | tf_op jit(solution)/shard_map/density/pallas_call | solution.py:381
  164.8 1.0 copy.11
  165.8 0.3 copy.16
  166.1 0.1 pad.4.clone
  166.2 0.3 reshape.17
  166.5 0.7 copy.14
  167.2 1.5 copy.19
  (1 shorter events, 0.0 us)

commit v4 on v3

--- a/solution.py
+++ b/solution.py
@@ -249,7 +249,9 @@
         pltpu.make_async_copy(outbox[index].at[me], landed[index].at[me], own_sem.at[index]).start()
 
         def send(hop, carry):
-            to = (me + peers // 2 + hop - 1 + hop // (peers // 2 + 1)) % peers
+            near_by = hop // (peers // 2 + 1)
+            place = (me + hop - 1 + near_by) % (peers // 2)
+            to = (((me // (peers // 2)) + 1 + near_by) % 2) * (peers // 2) + place
             pltpu.make_async_remote_copy(
                 src_ref=outbox[index].at[to], dst_ref=landed[index].at[me],
                 send_sem=send_sem.at[index], recv_sem=recv_sem.at[index],

time: 169 us -> 167 us (0.988)
  Pallas kernels: 164 us -> 162 us
    pallas_call x1, Pallas kernels: 164 us -> 162 us  [density_of(): pl.pallas_call(functools.partial(main_kernel, run, row_count, col_count),...]
where the time goes in v4:
time: 167 us; the launch traced here: 166 us
  Pallas kernels  162 us (97%)
  local copies, waits for them, and re-layouts  3.84 us (2%)
    pallas_call x1, Pallas kernels, density_of(): pl.pallas_call(functools.partial(main_kernel, run, row_count, col_count),...  162 us

profile of v4, /device:TPU:0, one launch (start us, length us, event | category | flops | bytes accessed | tf_op | source)
XLA Modules:
  0.0 166.4 jit_solution(5544733804640035885)
XLA Ops:
  0.6 161.9 %density.1 = (f32[2,2,4096]{2,1,0:T(2,128)}, f32[32,4,128]{2,1,0:T(4,128)}) custom-call(s32[2,7]{1,0:T(2,128)} %tile_list.1, s32[2]{0:T(128)} %tile_count.1, s32[2]{0:T(128)} %point_count.1, bf16[1536,3072]{1,0:T(8,128)(2,1)} %first.1, bf16[1536,3072]{1,0:T(8,128)(2,1)} %second.1, bf16[2,4096,896]{2,1,0:T(8,128)(2,1)} %basis.1, f32[3,2,4096]{2,1,0:T(2,128)} %offsets.1, ...), custom_call_target="tpu_custom_call" | custom-call | tf_op jit(solution)/shard_map/density/pallas_call | solution.py:383
  162.6 1.0 copy.11
  163.6 0.3 copy.16
  163.9 0.1 pad.4.clone
  163.9 0.3 reshape.17
  164.3 0.7 copy.14
  165.0 1.5 copy.19
  (1 shorter events, 0.0 us)
